TPU v7x, 32 devices: a whole 2x2x4 slice. The times are simulated.
32 devices in a mesh: seq: 8 (over y, x, core), head: 4 (over z).
Axes of the slice: x: 2, y: 2, z: 4, core: 2. Of those that a mesh axis runs over, the one named last changes fastest.
Arguments:
- queries: bfloat16 [8, 128, 8192], P('seq', None, 'head'), may hold values from -160 to 160
- continuation_key_slots: bfloat16 [8, 128, 1024], P('seq', None, 'head'), may hold values from -13.1875 to 13.1875
- continuation_value_slots: bfloat16 [8, 128, 1024], P('seq', None, 'head'), may hold values from -24 to 24
- cached_prompt_keys: bfloat16 [2, 8192, 1024], P(None, 'seq', 'head'), may hold values from -6 to 6
- cached_prompt_values: bfloat16 [2, 8192, 1024], P(None, 'seq', 'head'), may hold values from -24 to 24
- pair_lengths: int32 [2, 2], replicated, may hold values from 1 to 256
- prompt_of: int32 [2], replicated, may hold values from 0 to 1
- slot_tile: int32 [8], replicated, may hold values from 0 to 7, each once
- out_weight: bfloat16 [8192, 8192], P('head', 'seq'), may hold values from -0.0625 to 0.0625
Outputs:
- projected: bfloat16 [8, 128, 8192], P('head', None, 'seq')
Inputs may be any that keep to these rules, and one draw needn't show every extreme that they name: `slot_tile`: each of the 8 tiles stands in exactly one slot.
All inputs are finite; a program needn't handle non-finite values.
Results may differ from a plain program's by a relative error of at most 0.014.
Values may be sent and summed in bfloat16 or wider, within the bound.
A program may use at most 128 MiB of HBM per device.

v0:
```python
import math

import jax
import jax.numpy as jnp
from jax import lax
from jax.sharding import PartitionSpec as P

QUERY_HEADS = 64
KEY_VALUE_HEADS = 8
HEAD_WIDTH = 128
TILE_ROWS = 128
MAX_CONT_TILES = 2
PROMPT_COUNT = 2


VERY_LOW = -1e30


def tile_scores(query_tile, key_rows):
    raw = jnp.einsum("tkgd,pkd->kgtp", query_tile, key_rows, preferred_element_type=jnp.float32)
    return raw * (1.0 / math.sqrt(query_tile.shape[-1]))


def weigh_values(weights, value_rows):
    return jnp.einsum(
        "kgtp,pkd->kgtd",
        weights.astype(jnp.bfloat16),
        value_rows,
        preferred_element_type=jnp.float32,
    )


def local(
    queries,
    continuation_key_slots,
    continuation_value_slots,
    cached_prompt_keys,
    cached_prompt_values,
    pair_lengths,
    prompt_of,
    slot_tile,
    out_weight,
):
    seq_index = lax.axis_index("seq")
    slot_count = slot_tile.shape[0]
    tiles_here = queries.shape[0]
    kv_local = continuation_key_slots.shape[-1] // HEAD_WIDTH
    heads_per_group = QUERY_HEADS // KEY_VALUE_HEADS
    owner_slot = (
        jnp.zeros((slot_count,), jnp.int32)
        .at[slot_tile]
        .set(jnp.arange(slot_count, dtype=jnp.int32))
    )
    lengths = pair_lengths.reshape(-1)
    prompts = prompt_of[slot_tile // MAX_CONT_TILES // 2]
    local_q = queries.reshape(tiles_here, TILE_ROWS, kv_local, heads_per_group, HEAD_WIDTH)
    own_first = seq_index * tiles_here
    own_prompts = lax.dynamic_slice_in_dim(prompts, own_first, tiles_here, 0)
    start_state = (
        jnp.full((tiles_here, kv_local, heads_per_group, TILE_ROWS), VERY_LOW, jnp.float32),
        jnp.zeros((tiles_here, kv_local, heads_per_group, TILE_ROWS), jnp.float32),
        jnp.zeros((tiles_here, kv_local, heads_per_group, TILE_ROWS, HEAD_WIDTH), jnp.float32),
    )
    piece_keys = lax.all_gather(cached_prompt_keys, "seq", axis=1, tiled=True)
    piece_values = lax.all_gather(cached_prompt_values, "seq", axis=1, tiled=True)
    piece_rows = piece_keys.shape[1]
    block_rows = math.gcd(piece_rows, 1024)

    def one_block(block_id, inner):
        maxima_in, totals_in, weighted_in = inner
        block_keys = lax.dynamic_slice_in_dim(
            piece_keys, block_id * block_rows, block_rows, 1
        ).reshape(PROMPT_COUNT, block_rows, kv_local, HEAD_WIDTH)
        block_values = lax.dynamic_slice_in_dim(
            piece_values, block_id * block_rows, block_rows, 1
        ).reshape(PROMPT_COUNT, block_rows, kv_local, HEAD_WIDTH)
        key_rows = lax.dynamic_index_in_dim(block_keys, own_prompts[0], 0, False)
        value_rows = lax.dynamic_index_in_dim(block_values, own_prompts[0], 0, False)
        scores = tile_scores(local_q[0], key_rows)
        peak_new = jnp.maximum(maxima_in[0], jnp.max(scores, axis=3))
        weights = jnp.exp(scores - peak_new[..., None])
        keep = jnp.exp(maxima_in[0] - peak_new)
        total_new = totals_in[0] * keep + jnp.sum(weights, axis=3)
        weighted_new = weighted_in[0] * keep[..., None] + weigh_values(weights, value_rows)
        updated = [(peak_new, total_new, weighted_new)]
        return (
            jnp.stack([entry[0] for entry in updated]),
            jnp.stack([entry[1] for entry in updated]),
            jnp.stack([entry[2] for entry in updated]),
        )

    maxima, totals, weighted = lax.fori_loop(0, piece_rows // block_rows, one_block, start_state)
    all_keys, all_values = (
        lax.all_gather(continuation_key_slots, "seq", axis=0, tiled=True),
        lax.all_gather(continuation_value_slots, "seq", axis=0, tiled=True),
    )
    slot_index = own_first + 0
    tile_id = slot_tile[slot_index]
    continuation = tile_id // MAX_CONT_TILES
    offset = tile_id % MAX_CONT_TILES * TILE_ROWS
    place_indices = owner_slot[
        continuation * MAX_CONT_TILES + jnp.arange(MAX_CONT_TILES, dtype=jnp.int32)
    ]
    own_keys = all_keys[place_indices].reshape(MAX_CONT_TILES * TILE_ROWS, kv_local, HEAD_WIDTH)
    own_values = all_values[place_indices].reshape(MAX_CONT_TILES * TILE_ROWS, kv_local, HEAD_WIDTH)
    row_pos = offset + jnp.arange(TILE_ROWS, dtype=jnp.int32)
    col_pos = jnp.arange(MAX_CONT_TILES * TILE_ROWS, dtype=jnp.int32)
    causal = col_pos[None, :] <= row_pos[:, None]
    in_length = row_pos < lengths[continuation]
    scores = jnp.where(causal[None, None], tile_scores(local_q[0], own_keys), VERY_LOW)
    peak = jnp.maximum(maxima[0], jnp.max(scores, axis=3))
    weights = jnp.exp(scores - peak[..., None])
    rescale = jnp.exp(maxima[0] - peak)
    denominator = totals[0] * rescale + jnp.sum(weights, axis=3)
    numerator = weighted[0] * rescale[..., None] + weigh_values(weights, own_values)
    result = numerator / denominator[..., None]
    result = jnp.transpose(result, (2, 0, 1, 3)).reshape(
        TILE_ROWS, kv_local * heads_per_group * HEAD_WIDTH
    )
    outputs = [jnp.where(in_length[:, None], result, 0.0).astype(jnp.bfloat16)]
    attention = jnp.stack(outputs)
    partial_out = jnp.einsum(
        "stc,cd->std",
        lax.all_gather(attention, "seq", axis=0, tiled=True),
        out_weight,
        preferred_element_type=jnp.float32,
    )
    projected = lax.psum_scatter(
        partial_out.astype(jnp.bfloat16), "head", scatter_dimension=0, tiled=True
    )
    return projected


def solution(mesh):
    return jax.shard_map(
        local,
        mesh=mesh,
        in_specs=(
            P("seq", None, "head"),
            P("seq", None, "head"),
            P("seq", None, "head"),
            P(None, "seq", "head"),
            P(None, "seq", "head"),
            P(),
            P(),
            P(),
            P("head", "seq"),
        ),
        out_specs=P("head", None, "seq"),
        check_vma=False,
    )
```

profile of v0, /device:TPU:7, one launch (start us, length us, event | category | flops | bytes accessed | tf_op | source)
XLA Modules:
  0.0 282.3 jit_solution(15779046093581894624)
XLA Ops:
  6.6 2.3 copy.34
  9.0 2.3 copy.35
  18.6 12.0 %all_gather.17 = bf16[8,128,256]{2,1,0:T(8,128)(2,1)S(1)} all-gather(bf16[1,128,256]{2,1,0:T(8,128)(2,1)S(1)} %copy-done.2), channel_id=1, replica_groups=mesh['seq'=8,'head'=4] {'seq'}, dimensions={0}, use_global_device_ids=true | all-gather | bytes 589824 | tf_op jit(solution)/shard_map/all_gather | solution.py:94
  31.2 9.7 %all_gather.18 = bf16[8,128,256]{2,1,0:T(8,128)(2,1)S(1)} all-gather(bf16[1,128,256]{2,1,0:T(8,128)(2,1)S(1)} %copy-done.3), channel_id=1, replica_groups=mesh['seq'=8,'head'=4] {'seq'}, dimensions={0}, use_global_device_ids=true | all-gather | bytes 589824 | tf_op jit(solution)/shard_map/all_gather | solution.py:95
  43.5 1.8 fusion.43
  45.4 21.0 %all-gather.4.cloned.1.call-done = bf16[2,8192,256]{1,2,0:T(8,128)(2,1)} async-done(((bf16[2,1024,256]{1,2,0:T(8,128)(2,1)}), bf16[2,8192,256]{1,2,0:T(8,128)(2,1)}) %all-gather.4.cloned.1.call-update) | async-done | bytes 8388624 | tf_op jit(solution)/shard_map/all_gather | solution.py:64
  66.3 56.2 %all-gather.6.cloned.1.call-done = bf16[2,8192,256]{1,2,0:T(8,128)(2,1)} async-done(((bf16[2,1024,256]{1,2,0:T(8,128)(2,1)}), bf16[2,8192,256]{1,2,0:T(8,128)(2,1)}) %all-gather.6.cloned.1.call-update) | async-done | bytes 8388624 | tf_op jit(solution)/shard_map/all_gather | solution.py:65
  122.6 57.6 %while.20 = (s32[]{:T(128)}, f32[1,2,8,128]{3,2,1,0:T(8,128)S(1)}, f32[1,2,8,128]{3,2,1,0:T(8,128)S(1)}, f32[1,2,8,128,128]{4,3,2,1,0:T(8,128)S(1)}, bf16[2,8192...) while((s32[]{:T(128)}, f32[1,2,8,128]{3,2,1,0:T(8,128)S(1)}, ...), condition=%wide.region_3.4_spmd.clone, body=%wide.region_0.3_spmd.clone.sunk | while | flops 1091057664 | bytes 34201792 | solution.py:92
  122.8 1.7 constant_dynamic-slice_fusion.3
  125.8 2.6 fusion.54
  128.4 1.4 fusion.53
  130.0 1.7 constant_dynamic-slice_fusion.3
  133.0 2.6 fusion.54
  135.6 1.4 fusion.53
  137.2 1.7 constant_dynamic-slice_fusion.3
  140.2 2.6 fusion.54
  142.8 1.4 fusion.53
  144.3 1.7 constant_dynamic-slice_fusion.3
  147.4 2.6 fusion.54
  151.5 1.7 constant_dynamic-slice_fusion.3
  154.6 2.6 fusion.54
  158.7 1.7 constant_dynamic-slice_fusion.3
  161.8 2.6 fusion.54
  165.9 1.7 constant_dynamic-slice_fusion.3
  169.0 2.6 fusion.54
  173.1 1.7 constant_dynamic-slice_fusion.3
  176.2 2.6 fusion.54
  180.5 1.9 fusion.28
  182.5 2.1 fusion.30
  186.0 36.5 %all-gather.8.cloned.1.call-done = bf16[8,128,2048]{2,1,0:T(8,128)(2,1)} async-done(((bf16[1,128,2048]{2,1,0:T(8,128)(2,1)}), bf16[8,128,2048]{2,1,0:T(8,128)(2,1)}) %all-gather.8.cloned.1.call-update) | async-done | bytes 4194320 | tf_op jit(solution)/shard_map/all_gather | solution.py:124
  222.5 9.3 %fusion.25 = bf16[8,128,1024]{2,1,0:T(8,128)(2,1)} fusion(bf16[8,128,2048]{2,1,0:T(8,128)(2,1)} %all-gather.8.cloned.1.call-done, bf16[2048,1024]{1,0:T(8,128)(2,1)} %param.19), kind=kOutput, calls=%fused_computation.37 | convolution fusion | flops 4296015872 | bytes 10485760 | tf_op jit(solution)/shard_map/stc,cd->std/dot_general | solution.py:122
  231.8 43.9 %reduce-scatter.2.cloned.1.call-done = bf16[2,128,1024]{2,1,0:T(8,128)(2,1)} async-done(((bf16[8,128,1024]{2,1,0:T(8,128)(2,1)}), bf16[2,128,1024]{2,1,0:T(8,128)(2,1)}) %reduce-scatter.2.cloned.1.call-update) | async-done | bytes 524304 | tf_op jit(solution)/shard_map/reduce_scatter | solution.py:128
  (87 shorter events, 26.3 us)
Async XLA Ops:
  6.5 8.1 %copy-start = (s32[2]{0:T(128)S(1)}, s32[2]{0:T(128)}, u32[]{:S(2)}) copy-start(s32[2]{0:T(128)} %param.17) | copy-start | bytes 28
  6.5 4.8 %copy-start.5 = (s32[8]{0:T(128)S(1)}, s32[8]{0:T(128)}, u32[]{:S(2)}) copy-start(s32[8]{0:T(128)} %param.18) | copy-start | bytes 100
  6.5 10.7 %copy-start.4 = (s32[2,2]{1,0:T(2,128)S(1)}, s32[2,2]{1,0:T(2,128)}, u32[]{:S(2)}) copy-start(s32[2,2]{1,0:T(2,128)} %param.16) | copy-start | bytes 52
  6.5 12.0 %copy-start.2 = (bf16[1,128,256]{2,1,0:T(8,128)(2,1)S(1)}, bf16[1,128,256]{2,1,0:T(8,128)(2,1)}, u32[]{:S(2)}) copy-start(bf16[1,128,256]{2,1,0:T(8,128)(2,1)} %param.12) | copy-start | bytes 196612
  6.5 24.6 %copy-start.3 = (bf16[1,128,256]{2,1,0:T(8,128)(2,1)S(1)}, bf16[1,128,256]{2,1,0:T(8,128)(2,1)}, u32[]{:S(2)}) copy-start(bf16[1,128,256]{2,1,0:T(8,128)(2,1)} %param.13) | copy-start | bytes 196612
  6.5 59.8 %all-gather.4.cloned.1.call-start = ((), (), s32[]{:S(2)}) async-start(), calls=%async_computation.1 | async-start | bytes 9437184 | tf_op jit(solution)/shard_map/all_gather | solution.py:64
  8.9 32.5 %copy-start.1 = (bf16[1,128,2048]{2,1,0:T(8,128)(2,1)S(1)}, bf16[1,128,2048]{2,1,0:T(8,128)(2,1)}, u32[]{:S(2)}) copy-start(bf16[1,128,2048]{2,1,0:T(8,128)(2,1)} %param.11) | copy-start | bytes 1572868
  8.9 113.6 %all-gather.6.cloned.1.call-start = ((), (), s32[]{:S(2)}) async-start(), calls=%async_computation.2 | async-start | bytes 9437184 | tf_op jit(solution)/shard_map/all_gather | solution.py:65
  11.3 211.2 %all-gather.8.cloned.1.call-start = ((), (), s32[]{:S(2)}) async-start(), calls=%async_computation.3 | async-start | bytes 4718592 | tf_op jit(solution)/shard_map/all_gather | solution.py:124
  185.8 89.9 %reduce-scatter.2.cloned.1.call-start = ((), (), s32[]{:S(2)}) async-start(), calls=%async_computation.4 | async-start | bytes 2621440 | tf_op jit(solution)/shard_map/reduce_scatter | solution.py:128
Sparse Core Ops, SparseCore 0:
  9.3 57.0 all-gather.3
  68.2 54.2 all-gather.5
  185.9 36.5 all-gather.7
  231.9 43.7 reduce-scatter.1
where the time goes:
time: 285 us; the launch traced here: 282 us
  waiting for transfers between devices  158 us (55%)
  matrix products  44.4 us (16%)
  local copies, waits for them, and re-layouts  25 us (9%)
  blocking collectives  21.7 us (8%)
  between operations  17.9 us (6%)
  other arithmetic  14.7 us (5%)
    all_gather x1, waiting for transfers between devices, local(): lax.all_gather(cached_prompt_values, 'seq', axis=1, tiled=True)  56.2 us
    reduce_scatter x1, waiting for transfers between devices, local(): lax.psum_scatter(partial_out.astype(jnp.bfloat16), 'head', scatter_dimens...  43.9 us
    all_gather x1, waiting for transfers between devices, local(): lax.all_gather(attention, 'seq', axis=0, tiled=True)  36.5 us
    dot_general x9, matrix products, weigh_values(): jnp.einsum('kgtp,pkd->kgtd', weights.astype(jnp.bfloat16), value_rows, pr...  22.7 us
    all_gather x1, waiting for transfers between devices, local(): piece_keys = lax.all_gather(cached_prompt_keys, 'seq', axis=1, tiled=True)  21 us
    dynamic_slice x8, local copies, waits for them, and re-layouts, one_block(): lax.dynamic_slice_in_dim(piece_values, block_id * block_rows, block_rows, 1)  13.8 us
    dot_general x9, matrix products, tile_scores(): jnp.einsum('tkgd,pkd->kgtp', query_tile, key_rows, preferred_element_type...  12.4 us
    all_gather x1, blocking collectives, local(): lax.all_gather(continuation_key_slots, 'seq', axis=0, tiled=True)  12 us
  transfers between devices with their start and end apart: 4, of which 4 were waited for; matrix products, arithmetic and copies ran while one was open for 3% of the time, Pallas kernels for 0%

commit v1 on v0

v1 whole, which is shorter than its diff:
```python
import functools
import math

import jax
import jax.numpy as jnp
from jax import lax
from jax.experimental import pallas as pl
from jax.experimental.pallas import tpu as pltpu
from jax.sharding import PartitionSpec as P

QUERY_HEADS = 64
KEY_VALUE_HEADS = 8
HEAD_WIDTH = 128
TILE_ROWS = 128
MAX_CONT_TILES = 2
GROUP = QUERY_HEADS // KEY_VALUE_HEADS
LANES = 128
HALF = LANES // 2
VERY_LOW = -1e30
MESH = pl.DeviceIdType.MESH
EXP2_SCALE = math.log2(math.e) / math.sqrt(HEAD_WIDTH)


def flip(index, mask):
    return index + mask * (1 - 2 * (lax.rem(index // mask, 2)))


def chip_mask(step, core, bits):
    which = lax.rem(step + core, bits)
    return 2 * (1 + which + which * (which - 1) // 2)


def kernel(
    n,
    peers,
    q_hbm,
    kc_ref,
    vc_ref,
    k_ref,
    v_ref,
    lengths_ref,
    prompt_ref,
    tile_ref,
    w_hbm,
    out_ref,
    q_all,
    o_all,
    stats,
    o_core,
    st_core,
    o_chip,
    st_chip,
    attn,
    w_ref,
    share,
    arrived,
    local_sem,
    send_sem,
    recv_sem,
    z_send,
    z_recv,
):
    me = lax.axis_index("seq")
    z = lax.axis_index("head")
    core = lax.rem(me, 2)
    partner = flip(me, 1)
    half = n // 2
    bits = half.bit_length() - 1
    heads = q_hbm.shape[-1] // HEAD_WIDTH
    per_z = n // peers
    masks = [chip_mask(step, core, bits) for step in range(bits)]
    partner_masks = [chip_mask(step, 1 - core, bits) for step in range(bits)]
    mine, theirs = [me], [partner]
    for step in range(bits):
        mine += [flip(slot, masks[step]) for slot in mine]
        theirs += [flip(slot, partner_masks[step]) for slot in theirs]

    q_load = pltpu.make_async_copy(q_hbm.at[0], q_all.at[me], local_sem.at[0])
    w_load = pltpu.make_async_copy(w_hbm, w_ref, local_sem.at[1])
    q_load.start()
    w_load.start()
    barrier = pltpu.get_barrier_semaphore()
    neighbours = [(partner, z)] + [(flip(me, mask), z) for mask in masks]
    neighbours += [(me, lax.rem(z + hop, peers)) for hop in range(1, peers)]
    for device in neighbours:
        pl.semaphore_signal(barrier, inc=1, device_id=device, device_id_type=MESH)
    pl.semaphore_wait(barrier, len(neighbours))
    q_load.wait()

    counter = [0]
    sent = []

    def remote(src, dst, seq):
        index = counter[0]
        counter[0] += 1
        copy = pltpu.make_async_remote_copy(
            src_ref=src,
            dst_ref=dst,
            send_sem=send_sem.at[index],
            recv_sem=recv_sem.at[index],
            device_id=(seq, z),
            device_id_type=MESH,
        )
        sent.append(copy)
        return copy

    def gather(buf, use, flush):
        links = [
            [remote(buf.at[mine[j]], buf.at[mine[j]], flip(me, masks[step])) for j in range(2**step)]
            for step in range(bits)
        ]
        cores = [remote(buf.at[mine[j]], buf.at[mine[j]], partner) for j in range(half)]
        if bits:
            links[0][0].start()
        cores[0].start()
        use(mine[0])
        for step in range(1, bits):
            links[step][0].start()
        cores[0].wait_recv()
        use(theirs[0])
        flush(0)
        for step in range(bits):
            for j in range(2**step):
                slot = 2**step + j
                links[step][j].wait_recv()
                cores[slot].start()
                for later in range(step + 1, bits):
                    links[later][slot].start()
                use(mine[slot])
                cores[slot].wait_recv()
                use(theirs[slot])
                flush(slot)

    lane = lax.broadcasted_iota(jnp.int32, (TILE_ROWS, LANES), 1)
    row = lax.broadcasted_iota(jnp.int32, (TILE_ROWS, LANES), 0)
    own_tile = tile_ref[me]

    def attend(slot):
        tile = tile_ref[slot]
        prompt = prompt_ref[tile // MAX_CONT_TILES // 2]
        same = (tile // MAX_CONT_TILES) == (own_tile // MAX_CONT_TILES)
        shift = (tile % MAX_CONT_TILES - own_tile % MAX_CONT_TILES) * TILE_ROWS
        shift = jnp.where(same, shift, -1000000)
        allowed = (lane - row) <= shift
        allowed = jnp.concatenate([allowed.astype(jnp.float32)] * 2, axis=0) > 0.5
        stats[slot] = jnp.ones((TILE_ROWS, LANES), jnp.float32)
        contract = (((1,), (1,)), ((), ()))

        def block(step, carry):
            kv = (step * 4) // GROUP
            kv_lanes = pl.ds(pl.multiple_of(kv * HEAD_WIDTH, HEAD_WIDTH), HEAD_WIDTH)
            for part in range(2):
                head = step * 4 + part * 2
                lanes = [
                    pl.ds(pl.multiple_of((head + i) * HEAD_WIDTH, HEAD_WIDTH), HEAD_WIDTH)
                    for i in range(2)
                ]
                query = jnp.concatenate([q_all[slot, :, where] for where in lanes], axis=0)
                raw = lax.dot_general(
                    query, k_ref[prompt, :, kv_lanes], contract, preferred_element_type=jnp.float32
                )
                raw_own = lax.dot_general(
                    query, kc_ref[0, :, kv_lanes], contract, preferred_element_type=jnp.float32
                )
                raw_own = jnp.where(allowed, raw_own, VERY_LOW)
                peak = jnp.maximum(
                    jnp.max(raw, axis=1, keepdims=True), jnp.max(raw_own, axis=1, keepdims=True)
                )
                weights = jnp.exp2((raw - peak) * EXP2_SCALE).astype(jnp.bfloat16)
                weights_own = jnp.exp2((raw_own - peak) * EXP2_SCALE).astype(jnp.bfloat16)
                values = v_ref[prompt, :, kv_lanes]
                values_own = vc_ref[0, :, kv_lanes]
                both = jnp.dot(
                    weights,
                    jnp.concatenate([values, jnp.ones_like(values)], axis=1),
                    preferred_element_type=jnp.float32,
                ) + jnp.dot(
                    weights_own,
                    jnp.concatenate([values_own, jnp.ones_like(values_own)], axis=1),
                    preferred_element_type=jnp.float32,
                )
                total = both[:, HEAD_WIDTH:]
                out = (both[:, :HEAD_WIDTH] / total).astype(jnp.bfloat16)
                tile_stats = stats[slot]
                for i in range(2):
                    rows = slice(i * TILE_ROWS, (i + 1) * TILE_ROWS)
                    o_all[slot, :, lanes[i]] = out[rows]
                    tile_stats = jnp.where(lane == head + i, peak[rows], tile_stats)
                    tile_stats = jnp.where(lane == HALF + head + i, total[rows], tile_stats)
                stats[slot] = tile_stats
            return carry

        lax.fori_loop(0, heads // 4, block, 0)

    def merge(slot, other_o, other_st, store):
        one, two = stats[slot], other_st[...]
        top = jnp.maximum(one, two)
        share_one = jnp.exp2((one - top) * EXP2_SCALE) * pltpu.roll(one, HALF, 1)
        share_two = jnp.exp2((two - top) * EXP2_SCALE) * pltpu.roll(two, HALF, 1)
        total = share_one + share_two
        stats[slot] = jnp.where(lane < HALF, top, pltpu.roll(total, HALF, 1))
        share_one = share_one / total
        share_two = share_two / total
        for head in range(heads):
            lanes = slice(head * HEAD_WIDTH, (head + 1) * HEAD_WIDTH)
            store(
                lanes,
                o_all[slot, :, lanes].astype(jnp.float32) * share_one[:, head : head + 1]
                + other_o[:, lanes].astype(jnp.float32) * share_two[:, head : head + 1],
            )

    def keep(slot):
        def store(lanes, value):
            o_all[slot, :, lanes] = value.astype(jnp.bfloat16)

        return store

    to_core = []

    def attend_and_send(slot):
        attend(slot)

    def flush_core(j):
        del j

    def use_query(slot):
        attend(slot)
        if any(slot is other for other in theirs):
            j = [slot is other for other in theirs].index(True)
            pair = (
                remote(o_all.at[slot], o_core.at[j], partner),
                remote(stats.at[slot], st_core.at[j], partner),
            )
            for copy in pair:
                copy.start()
            to_core.append(pair)

    chip = {}

    def start_chip(step, j):
        slot = mine[2**step + j]
        base = 2**step - 1 + j
        pair = (
            remote(o_all.at[slot], o_chip.at[base], flip(me, masks[step])),
            remote(stats.at[slot], st_chip.at[base], flip(me, masks[step])),
        )
        for copy in pair:
            copy.start()
        chip[step, j] = pair

    def merge_core(j):
        for copy in to_core[j]:
            copy.wait_recv()
        merge(mine[j], o_core.at[j], st_core.at[j], keep(mine[j]))
        if bits and j >= 2 ** (bits - 1):
            start_chip(bits - 1, j - 2 ** (bits - 1))

    gather(q_all, use_query, merge_core)

    tile = own_tile
    continuation = tile // MAX_CONT_TILES
    length = lengths_ref[continuation // 2, continuation % 2]
    in_length = (tile % MAX_CONT_TILES) * TILE_ROWS + row < length

    def finish(lanes, value):
        attn[me, :, lanes] = jnp.where(in_length, value, 0.0).astype(jnp.bfloat16)

    for step in reversed(range(bits)):
        for j in reversed(range(2**step)):
            for copy in chip[step, j]:
                copy.wait_recv()
            base = 2**step - 1 + j
            last = step == 0
            merge(mine[j], o_chip.at[base], st_chip.at[base], finish if last else keep(mine[j]))
            if step and j >= 2 ** (step - 1):
                start_chip(step - 1, j - 2 ** (step - 1))

    w_load.wait()
    pending = []
    z_sent = []

    def use_attention(slot):
        pending.append(slot)

    def project(j):
        del j
        slots = [pending.pop(0), pending.pop(0)]
        rows = jnp.concatenate([attn[slot] for slot in slots], axis=0)
        product = jnp.dot(rows, w_ref[...], preferred_element_type=jnp.float32)
        product = product.astype(jnp.bfloat16)
        for i, slot in enumerate(slots):
            share[slot] = product[i * TILE_ROWS : (i + 1) * TILE_ROWS]
            owner, place = slot // per_z, lax.rem(slot, per_z)
            copy = pltpu.make_async_remote_copy(
                src_ref=share.at[slot],
                dst_ref=arrived.at[z, place],
                send_sem=z_send.at[slot],
                recv_sem=z_recv.at[z, place],
                device_id=(me, owner),
                device_id_type=MESH,
            )

            @pl.when(owner != z)
            def _(copy=copy):
                copy.start()

            z_sent.append((owner, copy))

    gather(attn, use_attention, project)

    totals = [share[z * per_z + place].astype(jnp.float32) for place in range(per_z)]
    for hop in range(1, peers):
        source = lax.rem(z + hop, peers)
        for place in range(per_z):
            pltpu.make_async_remote_copy(
                src_ref=share.at[z * per_z + place],
                dst_ref=arrived.at[source, place],
                send_sem=z_send.at[z * per_z + place],
                recv_sem=z_recv.at[source, place],
                device_id=(me, source),
                device_id_type=MESH,
            ).wait_recv()
            totals[place] += arrived[source, place].astype(jnp.float32)
    for place in range(per_z):
        out_ref[place] = totals[place].astype(out_ref.dtype)
    for copy in sent:
        copy.wait_send()
    for owner, copy in z_sent:

        @pl.when(owner != z)
        def _(copy=copy):
            copy.wait_send()


def local(n, peers, queries, kc, vc, keys, values, pair_lengths, prompt_of, slot_tile, out_weight):
    features = queries.shape[-1]
    columns = out_weight.shape[-1]
    half = n // 2
    bits = half.bit_length() - 1
    gathers = 2 * (half - 1 + half)
    copies = gathers + 2 * half + 2 * (half - 1)
    vmem = pl.BlockSpec(memory_space=pltpu.VMEM)
    smem = pl.BlockSpec(memory_space=pltpu.SMEM)
    hbm = pl.BlockSpec(memory_space=pl.ANY)
    slot = (TILE_ROWS, features)
    stat = (TILE_ROWS, LANES)
    scratch = [
        pltpu.VMEM((n, *slot), jnp.bfloat16),
        pltpu.VMEM((n, *slot), jnp.bfloat16),
        pltpu.VMEM((n, *stat), jnp.float32),
        pltpu.VMEM((half, *slot), jnp.bfloat16),
        pltpu.VMEM((half, *stat), jnp.float32),
        pltpu.VMEM((half, *slot), jnp.bfloat16),
        pltpu.VMEM((half, *stat), jnp.float32),
        pltpu.VMEM((n, *slot), jnp.bfloat16),
        pltpu.VMEM(out_weight.shape, jnp.bfloat16),
        pltpu.VMEM((n, TILE_ROWS, columns), jnp.bfloat16),
        pltpu.VMEM((peers, n // peers, TILE_ROWS, columns), jnp.bfloat16),
        pltpu.SemaphoreType.DMA((2,)),
        pltpu.SemaphoreType.DMA((copies,)),
        pltpu.SemaphoreType.DMA((copies,)),
        pltpu.SemaphoreType.DMA((n,)),
        pltpu.SemaphoreType.DMA((peers, n // peers)),
    ]
    return pl.pallas_call(
        functools.partial(kernel, n, peers),
        out_shape=jax.ShapeDtypeStruct((n // peers, TILE_ROWS, columns), jnp.bfloat16),
        in_specs=[hbm, vmem, vmem, vmem, vmem, smem, smem, smem, hbm],
        out_specs=vmem,
        scratch_shapes=scratch,
        compiler_params=pltpu.CompilerParams(
            collective_id=0, has_side_effects=True, vmem_limit_bytes=60 * 1024 * 1024
        ),
    )(queries, kc, vc, keys, values, pair_lengths, prompt_of, slot_tile, out_weight)


def solution(mesh):
    return jax.shard_map(
        functools.partial(local, mesh.shape["seq"], mesh.shape["head"]),
        mesh=mesh,
        in_specs=(
            P("seq", None, "head"),
            P("seq", None, "head"),
            P("seq", None, "head"),
            P(None, "seq", "head"),
            P(None, "seq", "head"),
            P(),
            P(),
            P(),
            P("head", "seq"),
        ),
        out_specs=P("head", None, "seq"),
        check_vma=False,
    )
```

time: 285 us -> 133 us (0.47)
  waiting for transfers between devices: 158 us -> 0 us
  Pallas kernels: 0 us -> 131 us
  matrix products: 44.4 us -> 0 us
  local copies, waits for them, and re-layouts: 25 us -> 1.87 us
  blocking collectives: 21.7 us -> 0 us
  between operations: 17.9 us -> 0.01 us
  other arithmetic: 14.7 us -> 0 us
    pallas_call x0 -> x1, Pallas kernels: none -> 131 us  [local(): pl.pallas_call(functools.partial(kernel, n, peers), out_shape=jax.ShapeDt...]
    all_gather x3 -> x0, waiting for transfers between devices: 114 us -> none  [the longest x1 56.2 us: local(): lax.all_gather(cached_prompt_values, 'seq', axis=1, tiled=True)]
    dot_general x19 -> x0, matrix products: 44.4 us -> none  [the longest x9 22.7 us: weigh_values(): jnp.einsum('kgtp,pkd->kgtd', weights.astype(jnp.bfloat16), value_rows, pr...]
    reduce_scatter x1 -> x0, waiting for transfers between devices: 43.9 us -> none  [local(): lax.psum_scatter(partial_out.astype(jnp.bfloat16), 'head', scatter_dimens...]
    all_gather x2 -> x0, blocking collectives: 21.7 us -> none  [the longest x1 12 us: local(): lax.all_gather(continuation_key_slots, 'seq', axis=0, tiled=True)]
    dynamic_slice x11 -> x0, local copies, waits for them, and re-layouts: 15.6 us -> none  [the longest x8 13.8 us: one_block(): lax.dynamic_slice_in_dim(piece_values, block_id * block_rows, block_rows, 1)]
    reduce_sum x9 -> x0, other arithmetic: 12.9 us -> none  [the longest x8 11 us: one_block(): total_new = totals_in[0] * keep + jnp.sum(weights, axis=3)]
    unnamed x15 -> x1, local copies, waits for them, and re-layouts: 4.76 us -> 1.87 us
  transfers between devices with their start and end apart: 4 -> 0, of which waited for: 4 -> 0; matrix products, arithmetic and copies ran while one was open for 3% -> 0% of each run, Pallas kernels for 0% -> 0%
where the time goes in v1:
time: 133 us
  Pallas kernels  131 us (98%)
  local copies, waits for them, and re-layouts  1.87 us (1%)
    pallas_call x1, Pallas kernels, local(): pl.pallas_call(functools.partial(kernel, n, peers), out_shape=jax.ShapeDt...  131 us

profile of v1, /device:TPU:7, one launch (start us, length us, event | category | flops | bytes accessed | tf_op | source)
XLA Modules:
  0.0 132.7 jit_solution(344796217558896504)
XLA Ops:
  0.0 130.8 %shard_map.91 = bf16[2,128,1024]{2,1,0:T(8,128)(2,1)} custom-call(bf16[1,128,2048]{2,1,0:T(8,128)(2,1)} %q_hbm.1, bf16[1,128,256]{2,1,0:T(8,128)(2,1)} %kc_ref.1, bf16[1,128,256]{2,1,0:T(8,128)(2,1)} %vc_ref.1, bf16[2,1024,256]{2,1,0:T(8,128)(2,1)} %k_ref.1, bf16[2,1024,256]{2,1,0:T(8,128)(2,1)} %v_ref.1, s32[2,2]{1,0:T(2,128)} %lengths_ref.1, s32[2]{0:T(128)} %prompt_ref.1, ...), custom_call_target="tpu_custom_call" | custom-call | tf_op jit(solution)/shard_map/pallas_call | solution.py:365
  130.8 1.9 %copy.11 = bf16[2,128,1024]{2,1,0:T(8,128)(2,1)} copy(bf16[2,128,1024]{2,1,0:T(8,128)(2,1)} %shard_map.91) | data formatting | bytes 1048576

commit v2 on v1

v2 whole, which is shorter than its diff:
```python
import functools
import math

import jax
import jax.numpy as jnp
from jax import lax
from jax.experimental import pallas as pl
from jax.experimental.pallas import tpu as pltpu
from jax.sharding import PartitionSpec as P

QUERY_HEADS = 64
KEY_VALUE_HEADS = 8
HEAD_WIDTH = 128
TILE_ROWS = 128
PARTS = 2
PART_ROWS = TILE_ROWS // PARTS
STACK = 4
MAX_CONT_TILES = 2
GROUP = QUERY_HEADS // KEY_VALUE_HEADS
LANES = 128
HALF = LANES // 2
VERY_LOW = -1e30
MESH = pl.DeviceIdType.MESH
EXP2_SCALE = math.log2(math.e) / math.sqrt(HEAD_WIDTH)


def flip(index, mask):
    return index + mask * (1 - 2 * (lax.rem(index // mask, 2)))


def chip_mask(step, core, bits):
    which = lax.rem(step + core, bits)
    return 2 * (1 + which + which * (which - 1) // 2)


def kernel(
    n,
    peers,
    q_hbm,
    kc_ref,
    vc_ref,
    k_ref,
    v_ref,
    lengths_ref,
    prompt_ref,
    tile_ref,
    w_hbm,
    out_ref,
    q_all,
    o_all,
    stats,
    o_core,
    st_core,
    o_chip,
    st_chip,
    attn,
    w_ref,
    share,
    arrived,
    local_sem,
    send_sem,
    recv_sem,
    z_send,
    z_recv,
):
    me = lax.axis_index("seq")
    z = lax.axis_index("head")
    core = lax.rem(me, 2)
    partner = flip(me, 1)
    half = n // 2
    bits = half.bit_length() - 1
    heads = q_hbm.shape[-1] // HEAD_WIDTH
    per_z = n // peers
    masks = [chip_mask(step, core, bits) for step in range(bits)]
    partner_masks = [chip_mask(step, 1 - core, bits) for step in range(bits)]
    mine, theirs = [me], [partner]
    for step in range(bits):
        mine += [flip(slot, masks[step]) for slot in mine]
        theirs += [flip(slot, partner_masks[step]) for slot in theirs]

    q_load = pltpu.make_async_copy(q_hbm.at[0], q_all.at[me], local_sem.at[0])
    w_load = pltpu.make_async_copy(w_hbm, w_ref, local_sem.at[1])
    q_load.start()
    w_load.start()
    barrier = pltpu.get_barrier_semaphore()
    neighbours = [(partner, z)] + [(flip(me, mask), z) for mask in masks]
    neighbours += [(me, lax.rem(z + hop, peers)) for hop in range(1, peers)]
    for device in neighbours:
        pl.semaphore_signal(barrier, inc=1, device_id=device, device_id_type=MESH)
    pl.semaphore_wait(barrier, len(neighbours))
    q_load.wait()

    counter = [0]
    sent = []

    def remote(src, dst, seq):
        index = counter[0]
        counter[0] += 1
        copy = pltpu.make_async_remote_copy(
            src_ref=src,
            dst_ref=dst,
            send_sem=send_sem.at[index],
            recv_sem=recv_sem.at[index],
            device_id=(seq, z),
            device_id_type=MESH,
        )
        sent.append(copy)
        return copy

    lane = lax.broadcasted_iota(jnp.int32, (PART_ROWS, LANES), 1)
    row = lax.broadcasted_iota(jnp.int32, (PART_ROWS, LANES), 0)
    own_tile = tile_ref[me]

    def attend(slot, part):
        rows = slice(part * PART_ROWS, (part + 1) * PART_ROWS)
        tile = tile_ref[slot]
        prompt = prompt_ref[tile // MAX_CONT_TILES // 2]
        same = (tile // MAX_CONT_TILES) == (own_tile // MAX_CONT_TILES)
        shift = (tile % MAX_CONT_TILES - own_tile % MAX_CONT_TILES) * TILE_ROWS
        shift = jnp.where(same, shift + part * PART_ROWS, -1000000)
        allowed = (lane - row) <= shift
        allowed = jnp.concatenate([allowed.astype(jnp.float32)] * STACK, axis=0) > 0.5
        stats[slot, rows] = jnp.ones((PART_ROWS, LANES), jnp.float32)
        contract = (((1,), (1,)), ((), ()))

        def block(kv, carry):
            kv_lanes = pl.ds(pl.multiple_of(kv * HEAD_WIDTH, HEAD_WIDTH), HEAD_WIDTH)
            for first in range(0, GROUP, STACK):
                head = kv * GROUP + first
                lanes = [
                    pl.ds(pl.multiple_of((head + i) * HEAD_WIDTH, HEAD_WIDTH), HEAD_WIDTH)
                    for i in range(STACK)
                ]
                query = jnp.concatenate([q_all[slot, rows, where] for where in lanes], axis=0)
                raw = lax.dot_general(
                    query, k_ref[prompt, :, kv_lanes], contract, preferred_element_type=jnp.float32
                )
                raw_own = lax.dot_general(
                    query, kc_ref[0, :, kv_lanes], contract, preferred_element_type=jnp.float32
                )
                raw_own = jnp.where(allowed, raw_own, VERY_LOW)
                peak = jnp.maximum(
                    jnp.max(raw, axis=1, keepdims=True), jnp.max(raw_own, axis=1, keepdims=True)
                )
                weights = jnp.exp2((raw - peak) * EXP2_SCALE).astype(jnp.bfloat16)
                weights_own = jnp.exp2((raw_own - peak) * EXP2_SCALE).astype(jnp.bfloat16)
                values = v_ref[prompt, :, kv_lanes]
                values_own = vc_ref[0, :, kv_lanes]
                both = jnp.dot(
                    weights,
                    jnp.concatenate([values, jnp.ones_like(values)], axis=1),
                    preferred_element_type=jnp.float32,
                ) + jnp.dot(
                    weights_own,
                    jnp.concatenate([values_own, jnp.ones_like(values_own)], axis=1),
                    preferred_element_type=jnp.float32,
                )
                total = both[:, HEAD_WIDTH:]
                out = (both[:, :HEAD_WIDTH] / total).astype(jnp.bfloat16)
                tile_stats = stats[slot, rows]
                for i in range(STACK):
                    of = slice(i * PART_ROWS, (i + 1) * PART_ROWS)
                    o_all[slot, rows, lanes[i]] = out[of]
                    tile_stats = jnp.where(lane == head + i, peak[of], tile_stats)
                    tile_stats = jnp.where(lane == HALF + head + i, total[of], tile_stats)
                stats[slot, rows] = tile_stats
            return carry

        lax.fori_loop(0, heads // GROUP, block, 0)

    class Part:
        def __init__(self, part):
            self.part = part
            self.rows = slice(part * PART_ROWS, (part + 1) * PART_ROWS)
            self.at = pl.ds(part * PART_ROWS, PART_ROWS)
            self.to_core = []
            self.chip = {}
            self.queries = self.routes(q_all)

        def routes(self, buf):
            def route(slot, seq):
                ref = buf.at[slot, self.at]
                return remote(ref, ref, seq)

            links = [
                [route(mine[j], flip(me, masks[step])) for j in range(2**step)]
                for step in range(bits)
            ]
            return links, [route(mine[j], partner) for j in range(half)]

        def begin(self, routes):
            links, cores = routes
            for step in range(bits):
                links[step][0].start()
            cores[0].start()

        def forward(self, routes, slot):
            links, cores = routes
            step = slot.bit_length() - 1
            links[step][slot - 2**step].wait_recv()
            cores[slot].start()
            for later in range(step + 1, bits):
                links[later][slot].start()

        def score(self, j):
            self.queries[1][j].wait_recv()
            attend(theirs[j], self.part)
            pair = (
                remote(o_all.at[theirs[j], self.at], o_core.at[j, self.at], partner),
                remote(stats.at[theirs[j], self.at], st_core.at[j, self.at], partner),
            )
            for copy in pair:
                copy.start()
            attend(mine[j], self.part)
            for copy in pair:
                copy.wait_recv()
            self.merge(mine[j], o_core, st_core, j, self.keep(mine[j]))
            if bits and j >= 2 ** (bits - 1):
                self.start_chip(bits - 1, j - 2 ** (bits - 1))

        def start_chip(self, step, j):
            slot = mine[2**step + j]
            base = 2**step - 1 + j
            to = flip(me, masks[step])
            pair = (
                remote(o_all.at[slot, self.at], o_chip.at[base, self.at], to),
                remote(stats.at[slot, self.at], st_chip.at[base, self.at], to),
            )
            for copy in pair:
                copy.start()
            self.chip[step, j] = pair

        def merge(self, slot, other_o, other_st, place, store):
            one, two = stats[slot, self.rows], other_st[place, self.rows]
            top = jnp.maximum(one, two)
            share_one = jnp.exp2((one - top) * EXP2_SCALE) * pltpu.roll(one, HALF, 1)
            share_two = jnp.exp2((two - top) * EXP2_SCALE) * pltpu.roll(two, HALF, 1)
            total = share_one + share_two
            stats[slot, self.rows] = jnp.where(lane < HALF, top, pltpu.roll(total, HALF, 1))
            share_one = share_one / total
            share_two = share_two / total
            for head in range(heads):
                lanes = slice(head * HEAD_WIDTH, (head + 1) * HEAD_WIDTH)
                store(
                    lanes,
                    o_all[slot, self.rows, lanes].astype(jnp.float32)
                    * share_one[:, head : head + 1]
                    + other_o[place, self.rows, lanes].astype(jnp.float32)
                    * share_two[:, head : head + 1],
                )

        def keep(self, slot):
            def store(lanes, value):
                o_all[slot, self.rows, lanes] = value.astype(jnp.bfloat16)

            return store

        def finish(self, lanes, value):
            continuation = own_tile // MAX_CONT_TILES
            length = lengths_ref[continuation // 2, continuation % 2]
            first = (own_tile % MAX_CONT_TILES) * TILE_ROWS + self.part * PART_ROWS
            value = jnp.where(first + row < length, value, 0.0)
            attn[me, self.rows, lanes] = value.astype(jnp.bfloat16)

        def project(self, slots):
            rows = jnp.concatenate([attn[slot, self.rows] for slot in slots], axis=0)
            product = jnp.dot(rows, w_ref[...], preferred_element_type=jnp.float32)
            product = product.astype(jnp.bfloat16)
            for i, slot in enumerate(slots):
                share[slot, self.rows] = product[i * PART_ROWS : (i + 1) * PART_ROWS]
                owner, place = slot // per_z, lax.rem(slot, per_z)
                copy = pltpu.make_async_remote_copy(
                    src_ref=share.at[slot, self.at],
                    dst_ref=arrived.at[z, place, self.at],
                    send_sem=z_send.at[self.part, slot],
                    recv_sem=z_recv.at[self.part, z, place],
                    device_id=(me, owner),
                    device_id_type=MESH,
                )

                @pl.when(owner != z)
                def _(copy=copy):
                    copy.start()

                z_sent.append((owner, copy))

        def after(self):
            for step in reversed(range(bits)):
                for j in reversed(range(2**step)):
                    for copy in self.chip[step, j]:
                        copy.wait_recv()
                    base = 2**step - 1 + j
                    store = self.finish if step == 0 else self.keep(mine[j])
                    self.merge(mine[j], o_chip, st_chip, base, store)
                    if step and j >= 2 ** (step - 1):
                        self.start_chip(step - 1, j - 2 ** (step - 1))
                if step:
                    yield
            routes = self.routes(attn)
            self.begin(routes)
            if self.part == 0:
                w_load.wait()
            yield
            slots = []
            for slot in range(half):
                if slot:
                    self.forward(routes, slot)
                    yield
                routes[1][slot].wait_recv()
                slots += [mine[slot], theirs[slot]]
                if True:
                    self.project(slots)
                    slots = []
                    yield

        def collect(self):
            totals = [
                share[z * per_z + place, self.rows].astype(jnp.float32) for place in range(per_z)
            ]
            for hop in range(1, peers):
                source = lax.rem(z + hop, peers)
                for place in range(per_z):
                    pltpu.make_async_remote_copy(
                        src_ref=share.at[z * per_z + place, self.at],
                        dst_ref=arrived.at[source, place, self.at],
                        send_sem=z_send.at[self.part, z * per_z + place],
                        recv_sem=z_recv.at[self.part, source, place],
                        device_id=(me, source),
                        device_id_type=MESH,
                    ).wait_recv()
                    totals[place] += arrived[source, place, self.rows].astype(jnp.float32)
            for place in range(per_z):
                out_ref[place, self.rows] = totals[place].astype(out_ref.dtype)

    z_sent = []
    early, late = Part(0), Part(1)
    early.begin(early.queries)
    late.begin(late.queries)
    early.score(0)
    for slot in range(1, half):
        early.forward(early.queries, slot)
        early.score(slot)
        late.forward(late.queries, slot)
    early_after, late_after = early.after(), late.after()
    for slot in range(half):
        late.score(slot)
        if slot:
            next(early_after, None)
    running = [early_after, late_after]
    while running:
        for one in list(running):
            try:
                next(one)
            except StopIteration:
                running.remove(one)
    early.collect()
    late.collect()
    for copy in sent:
        copy.wait_send()
    for owner, copy in z_sent:

        @pl.when(owner != z)
        def _(copy=copy):
            copy.wait_send()


def local(n, peers, queries, kc, vc, keys, values, pair_lengths, prompt_of, slot_tile, out_weight):
    features = queries.shape[-1]
    columns = out_weight.shape[-1]
    half = n // 2
    bits = half.bit_length() - 1
    gathers = 2 * (half - 1 + half)
    copies = PARTS * (gathers + 2 * half + 2 * (half - 1))
    vmem = pl.BlockSpec(memory_space=pltpu.VMEM)
    smem = pl.BlockSpec(memory_space=pltpu.SMEM)
    hbm = pl.BlockSpec(memory_space=pl.ANY)
    slot = (TILE_ROWS, features)
    stat = (TILE_ROWS, LANES)
    scratch = [
        pltpu.VMEM((n, *slot), jnp.bfloat16),
        pltpu.VMEM((n, *slot), jnp.bfloat16),
        pltpu.VMEM((n, *stat), jnp.float32),
        pltpu.VMEM((half, *slot), jnp.bfloat16),
        pltpu.VMEM((half, *stat), jnp.float32),
        pltpu.VMEM((half, *slot), jnp.bfloat16),
        pltpu.VMEM((half, *stat), jnp.float32),
        pltpu.VMEM((n, *slot), jnp.bfloat16),
        pltpu.VMEM(out_weight.shape, jnp.bfloat16),
        pltpu.VMEM((n, TILE_ROWS, columns), jnp.bfloat16),
        pltpu.VMEM((peers, n // peers, TILE_ROWS, columns), jnp.bfloat16),
        pltpu.SemaphoreType.DMA((2,)),
        pltpu.SemaphoreType.DMA((copies,)),
        pltpu.SemaphoreType.DMA((copies,)),
        pltpu.SemaphoreType.DMA((PARTS, n)),
        pltpu.SemaphoreType.DMA((PARTS, peers, n // peers)),
    ]
    return pl.pallas_call(
        functools.partial(kernel, n, peers),
        out_shape=jax.ShapeDtypeStruct((n // peers, TILE_ROWS, columns), jnp.bfloat16),
        in_specs=[hbm, vmem, vmem, vmem, vmem, smem, smem, smem, hbm],
        out_specs=vmem,
        scratch_shapes=scratch,
        compiler_params=pltpu.CompilerParams(
            collective_id=0, has_side_effects=True, vmem_limit_bytes=60 * 1024 * 1024
        ),
    )(queries, kc, vc, keys, values, pair_lengths, prompt_of, slot_tile, out_weight)


def solution(mesh):
    return jax.shard_map(
        functools.partial(local, mesh.shape["seq"], mesh.shape["head"]),
        mesh=mesh,
        in_specs=(
            P("seq", None, "head"),
            P("seq", None, "head"),
            P("seq", None, "head"),
            P(None, "seq", "head"),
            P(None, "seq", "head"),
            P(),
            P(),
            P(),
            P("head", "seq"),
        ),
        out_specs=P("head", None, "seq"),
        check_vma=False,
    )
```

time: 133 us -> 118 us (0.89); the launches traced: 133 us -> 116 us
  Pallas kernels: 131 us -> 114 us
    pallas_call x1, Pallas kernels: 131 us -> 114 us  [local(): pl.pallas_call(functools.partial(kernel, n, peers), out_shape=jax.ShapeDt...]
where the time goes in v2:
time: 118 us; the launch traced here: 116 us
  Pallas kernels  114 us (97%)
  local copies, waits for them, and re-layouts  1.87 us (2%)
    pallas_call x1, Pallas kernels, local(): pl.pallas_call(functools.partial(kernel, n, peers), out_shape=jax.ShapeDt...  114 us

profile of v2, /device:TPU:7, one launch (start us, length us, event | category | flops | bytes accessed | tf_op | source)
XLA Modules:
  0.0 116.1 jit_solution(3154393867166215140)
XLA Ops:
  0.0 114.2 %shard_map.91 = bf16[2,128,1024]{2,1,0:T(8,128)(2,1)} custom-call(bf16[1,128,2048]{2,1,0:T(8,128)(2,1)} %q_hbm.1, bf16[1,128,256]{2,1,0:T(8,128)(2,1)} %kc_ref.1, bf16[1,128,256]{2,1,0:T(8,128)(2,1)} %vc_ref.1, bf16[2,1024,256]{2,1,0:T(8,128)(2,1)} %k_ref.1, bf16[2,1024,256]{2,1,0:T(8,128)(2,1)} %v_ref.1, s32[2,2]{1,0:T(2,128)} %lengths_ref.1, s32[2]{0:T(128)} %prompt_ref.1, ...), custom_call_target="tpu_custom_call" | custom-call | tf_op jit(solution)/shard_map/pallas_call | solution.py:397
  114.3 1.9 %copy.11 = bf16[2,128,1024]{2,1,0:T(8,128)(2,1)} copy(bf16[2,128,1024]{2,1,0:T(8,128)(2,1)} %shard_map.91) | data formatting | bytes 1048576
